TPU v7x, 512 devices: a whole 4x8x8 slice. The times are simulated.
512 devices in a mesh: rows: 512 (over z, y, x, core).
Axes of the slice: x: 4, y: 8, z: 8, core: 2. Of those that a mesh axis runs over, the one named last changes fastest.
Arguments:
- adj_diag: int32 [8192, 512], P('rows'), may hold values from -2147483648 to 2147483647
- adj_right: int32 [8192, 512], P('rows'), may hold values from -2147483648 to 2147483647
- alive_diag: int32 [8192, 512], P('rows'), may hold values from -2147483648 to 2147483647
- alive_right: int32 [8192, 512], P('rows'), may hold values from -2147483648 to 2147483647
- truss_k: int32 [1], replicated, may hold values from 130 to 193
Outputs:
- support_field: float32 [262144, 1024], P('rows')
- removed_counts: int32 [3], replicated
All inputs are finite; a program needn't handle non-finite values.
Results may differ from a plain program's by a relative error of at most 0.0003.
Values may be sent and summed in bfloat16 or wider, within the bound.
No kernel may reach another device: no remote copies, remote signals or barrier semaphores. Data moves between devices by JAX's collectives and lax.ppermute only.
A program may use at most 64 MiB of HBM per device.

v0:
```python
import jax
import jax.numpy as jnp
from jax import lax
from jax.sharding import Mesh
from jax.sharding import PartitionSpec as P

ITERS = 3
ROWS = ("rows_0", "rows_1", "rows_2", "rows_3")


def shifted(array, axis, by):
    count = lax.axis_size(axis)
    return lax.ppermute(array, axis, [(i, (i + by) % count) for i in range(count)])


def over_axes(array, axes):
    for axis in axes:
        array = lax.psum(array, axis)
    return array


def unpack_tile(packed):
    shifts = jnp.arange(32, dtype=jnp.int32)
    tile_bits = packed[:, None, :] >> shifts[None, :, None] & 1
    return tile_bits.reshape(packed.shape[0] * 32, packed.shape[1])


def pack_bits(tile_bits):
    shifts = jnp.arange(32, dtype=jnp.int32)
    sectioned = tile_bits.reshape(tile_bits.shape[0] // 32, 32, tile_bits.shape[1])
    return jnp.sum(sectioned << shifts[None, :, None], axis=1, dtype=jnp.int32)


def within_tile(packed):
    upper_half = jnp.triu(unpack_tile(packed), 1)
    return (upper_half + upper_half.T).astype(jnp.bfloat16)


def across_tile(packed):
    return unpack_tile(packed).astype(jnp.bfloat16)


def pack_across(across):
    return pack_bits(across.astype(jnp.int32))


def fold_within(within):
    width = within.shape[0]
    half = width // 2
    row_ids = lax.broadcasted_iota(jnp.int32, (half, width), 0)
    col_ids = lax.broadcasted_iota(jnp.int32, (half, width), 1)
    flipped = within[half:][::-1, ::-1]
    folded = jnp.where(col_ids > row_ids, within[:half], flipped)
    return pack_bits(folded.astype(jnp.int32))


def unfold_within(packed):
    folded = unpack_tile(packed)
    half = folded.shape[0]
    width = folded.shape[1]
    row_ids = lax.broadcasted_iota(jnp.int32, (half, width), 0)
    col_ids = lax.broadcasted_iota(jnp.int32, (half, width), 1)
    top_rows = jnp.where(col_ids > row_ids, folded, jnp.zeros_like(folded))
    bottom_rows = jnp.where(col_ids < row_ids, folded, jnp.zeros_like(folded))[::-1, ::-1]
    upper_half = jnp.concatenate([top_rows, bottom_rows], axis=0)
    return (upper_half + upper_half.T).astype(jnp.bfloat16)


def support_within(prev_across, within, across):
    inside = lax.dot_general(
        prev_across, prev_across, (((0,), (0,)), ((), ())), preferred_element_type=jnp.float32
    )
    inside = inside + jnp.dot(within, within, preferred_element_type=jnp.float32)
    return inside + lax.dot_general(
        across, across, (((1,), (1,)), ((), ())), preferred_element_type=jnp.float32
    )


def support_across(within, across, next_within):
    between = jnp.dot(within, across, preferred_element_type=jnp.float32)
    return between + jnp.dot(across, next_within, preferred_element_type=jnp.float32)


def keep_edges(support, tile_mask, thresh):
    return jnp.where(support >= thresh, tile_mask, jnp.zeros_like(tile_mask))


def peel(prev_across, within, across, next_within, thresh):
    inside = support_within(prev_across, within, across)
    between = support_across(within, across, next_within)
    return (
        inside,
        between,
        keep_edges(inside, within, thresh),
        keep_edges(between, across, thresh),
    )


def tally(within, new_within, across, new_across):
    removed = jnp.sum((within - new_within).astype(jnp.int32)) // 2
    removed = removed + jnp.sum((across - new_across).astype(jnp.int32))
    return removed


def on_device(adj_diag, adj_right, alive_diag, alive_right, truss_k):
    within = within_tile(adj_diag & alive_diag)
    across_words = adj_right & alive_right
    across = across_tile(across_words)
    thresh = (truss_k[0] - 2).astype(jnp.float32)
    counts = []
    for step in range(ITERS):
        prev_across = across_tile(shifted(pack_across(across), ROWS, 1))
        next_within = unfold_within(shifted(fold_within(within), ROWS, -1))
        inside, between, new_within, new_across = peel(
            prev_across, within, across, next_within, thresh
        )
        counts.append(tally(within, new_within, across, new_across))
        within, across = (new_within, new_across)
    stacked = jnp.stack(counts)
    stacked = over_axes(stacked, ROWS)
    support = jnp.concatenate(
        [inside * within.astype(jnp.float32), between * across.astype(jnp.float32)], axis=1
    )
    return (support, stacked)


def solution(mesh):
    split = Mesh(mesh.devices.reshape(8, 8, 4, 2), ("rows_0", "rows_1", "rows_2", "rows_3"))
    placed = (P(ROWS, None), P(ROWS, None), P(ROWS, None), P(ROWS, None), P())
    return jax.shard_map(
        on_device, mesh=split, in_specs=placed, out_specs=(P(ROWS, None), P()), check_vma=False
    )
```

profile of v0, /device:TPU:1, one launch (start us, length us, event | category | flops | bytes accessed | tf_op | source)
XLA Modules:
  0.0 128.3 jit_solution(3447967203919431901)
XLA Ops:
  0.7 0.8 and.74
  2.4 0.9 rev.18
  3.5 8.7 %collective-permute-start.1 = (s32[8,512]{1,0:T(8,128)S(1)}, s32[8,512]{1,0:T(8,128)S(1)}, u32[]{:S(2)}, u32[]{:S(2)}) collective-permute-start(s32[8,512]{1,0:T(8,128)S(1)} %fusion.25), channel_id=1, source_target_pairs={{0,511},{1,0},{2,1},{3,2},{4,3},{5,4},{6,5},{7,6},{8,7},{9,8},{10,... | collective-permute-start | bytes 49160 | tf_op jit(solution)/shard_map/ppermute | solution.py:13
  12.6 1.9 %collective-permute-start = (s32[16,512]{1,0:T(8,128)S(1)}, s32[16,512]{1,0:T(8,128)S(1)}, u32[]{:S(2)}, u32[]{:S(2)}) collective-permute-start(s32[16,512]{1,0:T(8,128)S(1)} %get-tuple-element.9), channel_id=1, source_target_pairs={{0,1},{1,2},{2,3},{3,4},{4,5},{5,6},{6,7},{7,8},{8,9},{9,10},{10,1... | collective-permute-start | bytes 98312 | tf_op jit(solution)/shard_map/ppermute | solution.py:13
  14.6 1.4 %fusion.47 = f32[512,512]{1,0:T(8,128)} fusion(bf16[512,512]{1,0:T(8,128)(2,1)S(1)} %get-tuple-element.17, bf16[512,512]{1,0:T(8,128)(2,1)S(1)} %get-tuple-element.16), kind=kOutput, calls=%fused_computation.93 | convolution fusion | flops 268435456 | bytes 2097152 | tf_op jit(solution)/shard_map/dot_general | solution.py:80
  17.6 1.1 pad_add_fusion
  18.7 2.6 %copy.8 = s32[512,512]{0,1:T(8,128)} copy(s32[512,512]{1,0:T(8,128)} %pad_add_fusion) | data formatting | bytes 2097152 | tf_op jit(solution)/shard_map/concatenate | solution.py:65
  21.3 2.2 %fusion.8 = (s32[16,512]{1,0:T(8,128)S(1)}, bf16[512,512]{1,0:T(8,128)(2,1)S(1)}) fusion(bf16[512,512]{1,0:T(8,128)(2,1)S(1)} %get-tuple-element.16, f32[]{:T(128)} %bitcast.4, f32[512,512]{1,0:T(8,128)} %fusion.47, s32[512,512]{0,1:T(8,128)} %copy.8, s32[256,512]{1,0:T(8,128)S(1)} %rev.19, s32[256,512]{1,0:T(8,128)S(1)} %get-tuple-element.14), kind=kOutput, calls=%fused_computation.25 | convolution fusion | flops 270786560 | bytes 4227076 | tf_op jit(solution)/shard_map/dot_general | solution.py:81
  23.5 1.9 %collective-permute-start.4 = (s32[16,512]{1,0:T(8,128)S(1)}, s32[16,512]{1,0:T(8,128)S(1)}, u32[]{:S(2)}, u32[]{:S(2)}) collective-permute-start(s32[16,512]{1,0:T(8,128)S(1)} %get-tuple-element.20), channel_id=1, source_target_pairs={{0,1},{1,2},{2,3},{3,4},{4,5},{5,6},{6,7},{7,8},{8,9},{9,10},{10,1... | collective-permute-start | bytes 98312 | tf_op jit(solution)/shard_map/ppermute | solution.py:13
  26.9 0.9 rev.20
  28.0 10.1 %collective-permute-start.2 = (s32[8,512]{1,0:T(8,128)S(1)}, s32[8,512]{1,0:T(8,128)S(1)}, u32[]{:S(2)}, u32[]{:S(2)}) collective-permute-start(s32[8,512]{1,0:T(8,128)S(1)} %fusion.24), channel_id=1, source_target_pairs={{0,511},{1,0},{2,1},{3,2},{4,3},{5,4},{6,5},{7,6},{8,7},{9,8},{10,... | collective-permute-start | bytes 49160 | tf_op jit(solution)/shard_map/ppermute | solution.py:13
  39.6 0.9 rev.22
  40.6 9.1 %collective-permute-start.5 = (s32[8,512]{1,0:T(8,128)S(1)}, s32[8,512]{1,0:T(8,128)S(1)}, u32[]{:S(2)}, u32[]{:S(2)}) collective-permute-start(s32[8,512]{1,0:T(8,128)S(1)} %fusion.23), channel_id=1, source_target_pairs={{0,511},{1,0},{2,1},{3,2},{4,3},{5,4},{6,5},{7,6},{8,7},{9,8},{10,... | collective-permute-start | bytes 49160 | tf_op jit(solution)/shard_map/ppermute | solution.py:13
  49.7 1.4 %fusion.48 = f32[512,512]{1,0:T(8,128)} fusion(bf16[512,512]{1,0:T(8,128)(2,1)S(1)} %fusion.7, bf16[512,512]{1,0:T(8,128)(2,1)S(1)} %get-tuple-element.21), kind=kOutput, calls=%fused_computation.94 | convolution fusion | flops 268435456 | bytes 2097152 | tf_op jit(solution)/shard_map/dot_general | solution.py:80
  51.1 1.4 %fusion.28 = (s32[256,512]{1,0:T(8,128)}, s32[256,512]{1,0:T(8,128)}, s32[256,512]{1,0:T(8,128)}, s32[256,512]{1,0:T(8,128)S(1)}) fusion(s32[8,512]{1,0:T(8,128)S(1)} %collective-permute-done.5, s32[256]{0:T(256)S(1)} %shift_left.64, s32[8,512]{1,0:T(8,128)S(1)} %collective-permute-done.2), kind=kLoop, calls=%fused_computation.69 | loop fusion | flops 1310720 | bytes 2130944 | tf_op jit(solution)/shard_map/jit(_where)/select_n | solution.py:63
  52.5 3.9 %rev.21 = s32[256,512]{1,0:T(8,128)S(1)} reverse(s32[256,512]{1,0:T(8,128)} %get-tuple-element.18), dimensions={0,1} | reverse | bytes 1048576 | tf_op jit(solution)/shard_map/rev | solution.py:64
  56.4 1.1 pad_add_fusion.1
  57.5 2.6 %copy.9 = s32[512,512]{0,1:T(8,128)} copy(s32[512,512]{1,0:T(8,128)} %pad_add_fusion.1) | data formatting | bytes 2097152 | tf_op jit(solution)/shard_map/concatenate | solution.py:65
  60.1 2.4 %fusion.9 = (s32[16,512]{1,0:T(8,128)S(1)}, bf16[512,512]{1,0:T(8,128)(2,1)S(1)}) fusion(bf16[512,512]{1,0:T(8,128)(2,1)S(1)} %get-tuple-element.21, f32[]{:T(128)} %bitcast.4, f32[512,512]{1,0:T(8,128)} %fusion.48, s32[512,512]{0,1:T(8,128)} %copy.9, s32[256,512]{1,0:T(8,128)S(1)} %rev.21, s32[256,512]{1,0:T(8,128)} %copy-done.1), kind=kOutput, calls=%fused_computation.27 | convolution fusion | flops 270786560 | bytes 4227076 | tf_op jit(solution)/shard_map/dot_general | solution.py:81
  62.5 1.9 %collective-permute-start.3 = (s32[16,512]{1,0:T(8,128)S(1)}, s32[16,512]{1,0:T(8,128)S(1)}, u32[]{:S(2)}, u32[]{:S(2)}) collective-permute-start(s32[16,512]{1,0:T(8,128)S(1)} %get-tuple-element.24), channel_id=1, source_target_pairs={{0,1},{1,2},{2,3},{3,4},{4,5},{5,6},{6,7},{7,8},{8,9},{9,10},{10,1... | collective-permute-start | bytes 98312 | tf_op jit(solution)/shard_map/ppermute | solution.py:13
  64.4 3.8 %rev.23 = s32[256,512]{1,0:T(8,128)S(1)} reverse(s32[256,512]{1,0:T(8,128)} %get-tuple-element.11), dimensions={0,1} | reverse | bytes 1048576 | tf_op jit(solution)/shard_map/rev | solution.py:64
  68.2 2.1 %pad_add_fusion.2 = s32[512,512]{1,0:T(8,128)} fusion(s32[256,512]{1,0:T(8,128)S(1)} %rev.23, s32[256,512]{1,0:T(8,128)} %get-tuple-element.10), kind=kLoop, calls=%fused_computation.23 | loop fusion | flops 262144 | bytes 2097152 | tf_op jit(solution)/shard_map/concatenate | solution.py:65
  70.3 2.5 %copy.13 = s32[512,512]{0,1:T(8,128)} copy(s32[512,512]{1,0:T(8,128)} %pad_add_fusion.2) | data formatting | bytes 2097152 | tf_op jit(solution)/shard_map/concatenate | solution.py:65
  74.2 1.5 %convert_multiply_fusion = (f32[512,512]{1,0:T(8,128)}, f32[512,512]{1,0:T(8,128)S(1)}) fusion(bf16[512,512]{1,0:T(8,128)(2,1)S(1)} %get-tuple-element.25, f32[]{:T(128)} %bitcast.4, f32[512,512]{1,0:T(8,128)S(1)} %fusion.49, s32[512,512]{0,1:T(8,128)S(1)} %copy-done.3, s32[256,512]{1,0:T(8,128)S(1)} %rev.23, s32[256,512]{1,0:T(8,128)S(1)} %copy-done), kind=kOutput, calls=%fused_computation.48 | convolution fusion | flops 270532608 | bytes 5767172 | tf_op jit(solution)/shard_map/dot_general | solution.py:81
  75.7 1.5 %convert_reduce_fusion.4 = (s32[]{:T(128)}, s32[]{:T(128)}, s32[]{:T(128)}) fusion(bf16[512,512]{1,0:T(8,128)(2,1)S(1)} %get-tuple-element.21, s32[512]{0:T(512)S(1)} %shift_right_arithmetic.162, s32[16,512]{1,0:T(8,128)S(1)} %and.71, bf16[512,512]{1,0:T(8,128)(2,1)S(1)} %get-tuple-element.25, f32[512,512]{1,0:T(8,128)S(1)} %get-tuple-element.23, f32[]{:T(128)} %bitcast.4), kind=kLoop, calls=%fused_computation.46 | loop fusion | flops 4718589 | bytes 2131984 | tf_op jit(solution)/shard_map/reduce_sum | solution.py:101
  78.1 1.5 %convert_multiply_fusion.1 = (f32[512,512]{1,0:T(8,128)}, f32[512,512]{1,0:T(8,128)S(1)}) fusion(bf16[512,512]{1,0:T(8,128)(2,1)S(1)} %fusion.6, f32[]{:T(128)} %bitcast.4, f32[512,512]{1,0:T(8,128)S(1)} %convolution_add_fusion.2, bf16[512,512]{1,0:T(8,128)(2,1)S(1)} %get-tuple-element.25), kind=kOutput, calls=%fused_computation.49 | convolution fusion | flops 269746176 | bytes 4194308 | tf_op jit(solution)/shard_map/dot_general | solution.py:74
  79.6 1.4 %convert_reduce_fusion.5 = (s32[]{:T(128)}, s32[]{:T(128)}, s32[]{:T(128)}) fusion(bf16[512,512]{1,0:T(8,128)(2,1)S(1)} %get-tuple-element.17, bf16[512,512]{1,0:T(8,128)(2,1)S(1)} %fusion.7, bf16[512,512]{1,0:T(8,128)(2,1)S(1)} %fusion.6, f32[512,512]{1,0:T(8,128)S(1)} %get-tuple-element.27, f32[]{:T(128)} %bitcast.4), kind=kLoop, calls=%fused_computation.47 | loop fusion | flops 2883581 | bytes 2621456 | tf_op jit(solution)/shard_map/reduce_sum | solution.py:100
  90.5 7.0 %psum.28 = s32[3]{0:T(128)S(1)} all-reduce(s32[3]{0:T(128)S(1)} %pad_add_fusion.3), channel_id=1, replica_groups=mesh['rows_0'=8,'rows_1'=8,'rows_2'=4,'rows_3'=2] {'rows_0'}, use_global_device_ids=true, to_apply=%region_12.13 | all-reduce | flops 3 | bytes 24 | tf_op jit(solution)/shard_map/psum | solution.py:18
  97.5 7.0 %psum.29 = s32[3]{0:T(128)S(1)} all-reduce(s32[3]{0:T(128)S(1)} %psum.28), channel_id=1, replica_groups=mesh['rows_0'=8,'rows_1'=8,'rows_2'=4,'rows_3'=2] {'rows_1'}, use_global_device_ids=true, to_apply=%region_13.14 | all-reduce | flops 3 | bytes 24 | tf_op jit(solution)/shard_map/psum | solution.py:18
  104.5 11.6 %psum.30 = s32[3]{0:T(128)S(1)} all-reduce(s32[3]{0:T(128)S(1)} %psum.29), channel_id=1, replica_groups=mesh['rows_0'=8,'rows_1'=8,'rows_2'=4,'rows_3'=2] {'rows_2'}, use_global_device_ids=true, to_apply=%region_14.15 | all-reduce | flops 3 | bytes 24 | tf_op jit(solution)/shard_map/psum | solution.py:18
  116.1 9.4 %psum.31 = s32[3]{0:T(128)} all-reduce(s32[3]{0:T(128)S(1)} %psum.30), channel_id=1, replica_groups=mesh['rows_0'=8,'rows_1'=8,'rows_2'=4,'rows_3'=2] {'rows_3'}, use_global_device_ids=true, to_apply=%region_15.16 | all-reduce | flops 3 | bytes 24 | tf_op jit(solution)/shard_map/psum | solution.py:18
  125.5 2.8 %pad_maximum_fusion = f32[512,1024]{1,0:T(8,128)} fusion(f32[512,512]{1,0:T(8,128)} %get-tuple-element.22, f32[512,512]{1,0:T(8,128)S(1)} %copy-done.2), kind=kLoop, calls=%fused_computation | loop fusion | flops 524288 | bytes 4194304 | tf_op jit(solution)/shard_map/concatenate | solution.py:121
  (45 shorter events, 8.0 us)
Async XLA Ops:
  0.6 1.4 %copy-start.4 = (s32[16,512]{1,0:T(8,128)S(1)}, s32[16,512]{1,0:T(8,128)}, u32[]{:S(2)}) copy-start(s32[16,512]{1,0:T(8,128)} %param.6) | copy-start | bytes 98308
  0.6 1.4 %copy-start.5 = (s32[16,512]{1,0:T(8,128)S(1)}, s32[16,512]{1,0:T(8,128)}, u32[]{:S(2)}) copy-start(s32[16,512]{1,0:T(8,128)} %param.8) | copy-start | bytes 98308
  3.5 13.2 %collective-permute-start.1 = (s32[8,512]{1,0:T(8,128)S(1)}, s32[8,512]{1,0:T(8,128)S(1)}, u32[]{:S(2)}, u32[]{:S(2)}) collective-permute-start(s32[8,512]{1,0:T(8,128)S(1)} %fusion.25), channel_id=1, source_target_pairs={{0,511},{1,0},{2,1},{3,2},{4,3},{5,4},{6,5},{7,6},{8,7},{9,8},{10,... | collective-permute-start | bytes 49160 | tf_op jit(solution)/shard_map/ppermute | solution.py:13
  12.6 12.8 %collective-permute-start = (s32[16,512]{1,0:T(8,128)S(1)}, s32[16,512]{1,0:T(8,128)S(1)}, u32[]{:S(2)}, u32[]{:S(2)}) collective-permute-start(s32[16,512]{1,0:T(8,128)S(1)} %get-tuple-element.9), channel_id=1, source_target_pairs={{0,1},{1,2},{2,3},{3,4},{4,5},{5,6},{6,7},{7,8},{8,9},{9,10},{10,1... | collective-permute-start | bytes 98312 | tf_op jit(solution)/shard_map/ppermute | solution.py:13
  23.5 14.6 %collective-permute-start.4 = (s32[16,512]{1,0:T(8,128)S(1)}, s32[16,512]{1,0:T(8,128)S(1)}, u32[]{:S(2)}, u32[]{:S(2)}) collective-permute-start(s32[16,512]{1,0:T(8,128)S(1)} %get-tuple-element.20), channel_id=1, source_target_pairs={{0,1},{1,2},{2,3},{3,4},{4,5},{5,6},{6,7},{7,8},{8,9},{9,10},{10,1... | collective-permute-start | bytes 98312 | tf_op jit(solution)/shard_map/ppermute | solution.py:13
  28.0 23.1 %collective-permute-start.2 = (s32[8,512]{1,0:T(8,128)S(1)}, s32[8,512]{1,0:T(8,128)S(1)}, u32[]{:S(2)}, u32[]{:S(2)}) collective-permute-start(s32[8,512]{1,0:T(8,128)S(1)} %fusion.24), channel_id=1, source_target_pairs={{0,511},{1,0},{2,1},{3,2},{4,3},{5,4},{6,5},{7,6},{8,7},{9,8},{10,... | collective-permute-start | bytes 49160 | tf_op jit(solution)/shard_map/ppermute | solution.py:13
  40.6 10.5 %collective-permute-start.5 = (s32[8,512]{1,0:T(8,128)S(1)}, s32[8,512]{1,0:T(8,128)S(1)}, u32[]{:S(2)}, u32[]{:S(2)}) collective-permute-start(s32[8,512]{1,0:T(8,128)S(1)} %fusion.23), channel_id=1, source_target_pairs={{0,511},{1,0},{2,1},{3,2},{4,3},{5,4},{6,5},{7,6},{8,7},{9,8},{10,... | collective-permute-start | bytes 49160 | tf_op jit(solution)/shard_map/ppermute | solution.py:13
  52.5 5.0 %copy-start.1 = (s32[256,512]{1,0:T(8,128)}, s32[256,512]{1,0:T(8,128)S(1)}, u32[]{:S(2)}) copy-start(s32[256,512]{1,0:T(8,128)S(1)} %get-tuple-element.19) | copy-start | bytes 1572868
  62.5 14.7 %collective-permute-start.3 = (s32[16,512]{1,0:T(8,128)S(1)}, s32[16,512]{1,0:T(8,128)S(1)}, u32[]{:S(2)}, u32[]{:S(2)}) collective-permute-start(s32[16,512]{1,0:T(8,128)S(1)} %get-tuple-element.24), channel_id=1, source_target_pairs={{0,1},{1,2},{2,3},{3,4},{4,5},{5,6},{6,7},{7,8},{8,9},{9,10},{10,1... | collective-permute-start | bytes 98312 | tf_op jit(solution)/shard_map/ppermute | solution.py:13
  72.8 1.0 copy-start
  72.8 1.4 %copy-start.3 = (s32[512,512]{0,1:T(8,128)S(1)}, s32[512,512]{0,1:T(8,128)}, u32[]{:S(2)}) copy-start(s32[512,512]{0,1:T(8,128)} %copy.13) | copy-start | bytes 3145732
  79.6 45.9 %copy-start.2 = (f32[512,512]{1,0:T(8,128)S(1)}, f32[512,512]{1,0:T(8,128)}, u32[]{:S(2)}) copy-start(f32[512,512]{1,0:T(8,128)} %get-tuple-element.26) | copy-start | bytes 3145732
where the time goes:
time: 129 us; the launch traced here: 128 us
  blocking collectives  35 us (27%)
  starting transfers between devices  33.7 us (26%)
  local copies, waits for them, and re-layouts  20.4 us (16%)
  matrix products  14.6 us (11%)
  other arithmetic  13.6 us (11%)
  between operations  11.1 us (9%)
    psum x4, blocking collectives, over_axes(): array = lax.psum(array, axis)  35 us
    ppermute x6, starting transfers between devices, shifted(): lax.ppermute(array, axis, [(i, (i + by) % count) for i in range(count)])  33.7 us
    rev x3, local copies, waits for them, and re-layouts, unfold_within(): jnp.where(col_ids < row_ids, folded, jnp.zeros_like(folded))[::-1, ::-1]  8.42 us
    concatenate x3, local copies, waits for them, and re-layouts, unfold_within(): upper_half = jnp.concatenate([top_rows, bottom_rows], axis=0)  7.69 us
    dot_general x3, matrix products, support_across(): jnp.dot(across, next_within, preferred_element_type=jnp.float32)  6.13 us
    concatenate x3, other arithmetic, unfold_within(): upper_half = jnp.concatenate([top_rows, bottom_rows], axis=0)  4.27 us
    dot_general x3, matrix products, support_across(): between = jnp.dot(within, across, preferred_element_type=jnp.float32)  3.25 us
    concatenate x1, other arithmetic, on_device(): jnp.concatenate([inside * within.astype(jnp.float32), between * across.as...  2.76 us
  transfers between devices with their start and end apart: 6, of which 0 were waited for; matrix products, arithmetic and copies ran while one was open for 21% of the time, Pallas kernels for 0%

commit v1 on v0

--- a/solution.py
+++ b/solution.py
@@ -3,6 +3,7 @@
 from jax import lax
 from jax.sharding import Mesh
 from jax.sharding import PartitionSpec as P
+from jax.lax import all_gather
 
 ITERS = 3
 ROWS = ("rows_0", "rows_1", "rows_2", "rows_3")
@@ -15,7 +16,11 @@
 
 def over_axes(array, axes):
     for axis in axes:
-        array = lax.psum(array, axis)
+
+        def _hold_units(inp, ax_name):
+            return jnp.sum(all_gather(inp, ax_name), 0)
+
+        array = _hold_units(array, axis)
     return array
 
 

time: 129 us -> 139 us (1.078)
  local copies, waits for them, and re-layouts: 20.4 us -> 26.6 us
  between operations: 11.1 us -> 13.6 us
    psum x4 -> x0, blocking collectives: 35 us -> none  [over_axes(): array = lax.psum(array, axis)]
    unnamed x0 -> x4, blocking collectives: none -> 34.5 us
    unnamed x12 -> x23, local copies, waits for them, and re-layouts: 0.97 us -> 6.92 us
  transfers between devices with their start and end apart: 6 -> 6, of which waited for: 0 -> 0; matrix products, arithmetic and copies ran while one was open for 21% -> 23% of each run, Pallas kernels for 0% -> 0%
where the time goes in v1:
time: 139 us; the launch traced here: 137 us
  blocking collectives  34.5 us (25%)
  starting transfers between devices  33.7 us (24%)
  local copies, waits for them, and re-layouts  26.6 us (19%)
  matrix products  14.6 us (11%)
  other arithmetic  14.3 us (10%)
  between operations  13.6 us (10%)
    unnamed x4, blocking collectives  34.5 us
    ppermute x6, starting transfers between devices, shifted(): lax.ppermute(array, axis, [(i, (i + by) % count) for i in range(count)])  33.7 us
    rev x3, local copies, waits for them, and re-layouts, unfold_within(): jnp.where(col_ids < row_ids, folded, jnp.zeros_like(folded))[::-1, ::-1]  8.42 us
    concatenate x3, local copies, waits for them, and re-layouts, unfold_within(): upper_half = jnp.concatenate([top_rows, bottom_rows], axis=0)  7.69 us
    unnamed x23, local copies, waits for them, and re-layouts  6.92 us
    dot_general x3, matrix products, support_across(): jnp.dot(across, next_within, preferred_element_type=jnp.float32)  6.13 us
    concatenate x3, other arithmetic, unfold_within(): upper_half = jnp.concatenate([top_rows, bottom_rows], axis=0)  4.27 us
    dot_general x3, matrix products, support_across(): between = jnp.dot(within, across, preferred_element_type=jnp.float32)  3.25 us
  transfers between devices with their start and end apart: 6, of which 0 were waited for; matrix products, arithmetic and copies ran while one was open for 23% of the time, Pallas kernels for 0%

profile of v1, /device:TPU:1, one launch (start us, length us, event | category | flops | bytes accessed | tf_op | source)
XLA Modules:
  0.0 137.3 jit_solution(16279163036087495224)
XLA Ops:
  3.5 8.7 %collective-permute-start.1 = (s32[8,512]{1,0:T(8,128)S(1)}, s32[8,512]{1,0:T(8,128)S(1)}, u32[]{:S(2)}, u32[]{:S(2)}) collective-permute-start(s32[8,512]{1,0:T(8,128)S(1)} %fusion.25), channel_id=1, source_target_pairs={{0,511},{1,0},{2,1},{3,2},{4,3},{5,4},{6,5},{7,6},{8,7},{9,8},{10,... | collective-permute-start | bytes 49160 | tf_op jit(solution)/shard_map/ppermute | solution.py:14
  12.6 1.9 %collective-permute-start = (s32[16,512]{1,0:T(8,128)S(1)}, s32[16,512]{1,0:T(8,128)S(1)}, u32[]{:S(2)}, u32[]{:S(2)}) collective-permute-start(s32[16,512]{1,0:T(8,128)S(1)} %get-tuple-element.9), channel_id=1, source_target_pairs={{0,1},{1,2},{2,3},{3,4},{4,5},{5,6},{6,7},{7,8},{8,9},{9,10},{10,1... | collective-permute-start | bytes 98312 | tf_op jit(solution)/shard_map/ppermute | solution.py:14
  14.6 1.4 %fusion.47 = f32[512,512]{1,0:T(8,128)} fusion(bf16[512,512]{1,0:T(8,128)(2,1)S(1)} %get-tuple-element.17, bf16[512,512]{1,0:T(8,128)(2,1)S(1)} %get-tuple-element.16), kind=kOutput, calls=%fused_computation.93 | convolution fusion | flops 268435456 | bytes 2097152 | tf_op jit(solution)/shard_map/dot_general | solution.py:85
  16.7 1.3 dynamic-slice
  18.1 1.3 dynamic-slice.1
  20.7 1.3 dynamic-slice.2
  22.6 1.3 dynamic-slice.3
  24.8 1.1 pad_add_fusion
  25.9 2.6 %copy.17 = s32[512,512]{0,1:T(8,128)} copy(s32[512,512]{1,0:T(8,128)} %pad_add_fusion) | data formatting | bytes 2097152 | tf_op jit(solution)/shard_map/concatenate | solution.py:70
  28.5 2.2 %fusion.8 = (s32[16,512]{1,0:T(8,128)S(1)}, bf16[512,512]{1,0:T(8,128)(2,1)S(1)}) fusion(bf16[512,512]{1,0:T(8,128)(2,1)S(1)} %get-tuple-element.16, f32[]{:T(128)} %bitcast.4, f32[512,512]{1,0:T(8,128)} %fusion.47, s32[512,512]{0,1:T(8,128)} %copy.17, s32[256,512]{1,0:T(8,128)S(1)} %rev.19, s32[256,512]{1,0:T(8,128)S(1)} %get-tuple-element.14), kind=kOutput, calls=%fused_computation.25 | convolution fusion | flops 270786560 | bytes 4227076 | tf_op jit(solution)/shard_map/dot_general | solution.py:86
  30.7 1.9 %collective-permute-start.4 = (s32[16,512]{1,0:T(8,128)S(1)}, s32[16,512]{1,0:T(8,128)S(1)}, u32[]{:S(2)}, u32[]{:S(2)}) collective-permute-start(s32[16,512]{1,0:T(8,128)S(1)} %get-tuple-element.20), channel_id=1, source_target_pairs={{0,1},{1,2},{2,3},{3,4},{4,5},{5,6},{6,7},{7,8},{8,9},{9,10},{10,1... | collective-permute-start | bytes 98312 | tf_op jit(solution)/shard_map/ppermute | solution.py:14
  35.2 10.1 %collective-permute-start.2 = (s32[8,512]{1,0:T(8,128)S(1)}, s32[8,512]{1,0:T(8,128)S(1)}, u32[]{:S(2)}, u32[]{:S(2)}) collective-permute-start(s32[8,512]{1,0:T(8,128)S(1)} %fusion.24), channel_id=1, source_target_pairs={{0,511},{1,0},{2,1},{3,2},{4,3},{5,4},{6,5},{7,6},{8,7},{9,8},{10,... | collective-permute-start | bytes 49160 | tf_op jit(solution)/shard_map/ppermute | solution.py:14
  47.8 9.1 %collective-permute-start.5 = (s32[8,512]{1,0:T(8,128)S(1)}, s32[8,512]{1,0:T(8,128)S(1)}, u32[]{:S(2)}, u32[]{:S(2)}) collective-permute-start(s32[8,512]{1,0:T(8,128)S(1)} %fusion.23), channel_id=1, source_target_pairs={{0,511},{1,0},{2,1},{3,2},{4,3},{5,4},{6,5},{7,6},{8,7},{9,8},{10,... | collective-permute-start | bytes 49160 | tf_op jit(solution)/shard_map/ppermute | solution.py:14
  56.9 1.4 %fusion.48 = f32[512,512]{1,0:T(8,128)} fusion(bf16[512,512]{1,0:T(8,128)(2,1)S(1)} %fusion.7, bf16[512,512]{1,0:T(8,128)(2,1)S(1)} %get-tuple-element.21), kind=kOutput, calls=%fused_computation.94 | convolution fusion | flops 268435456 | bytes 2097152 | tf_op jit(solution)/shard_map/dot_general | solution.py:85
  58.3 1.4 %fusion.28 = (s32[256,512]{1,0:T(8,128)}, s32[256,512]{1,0:T(8,128)}, s32[256,512]{1,0:T(8,128)}, s32[256,512]{1,0:T(8,128)S(1)}) fusion(s32[8,512]{1,0:T(8,128)S(1)} %collective-permute-done.5, s32[256]{0:T(256)S(1)} %shift_left.64, s32[8,512]{1,0:T(8,128)S(1)} %collective-permute-done.2), kind=kLoop, calls=%fused_computation.69 | loop fusion | flops 1310720 | bytes 2130944 | tf_op jit(solution)/shard_map/jit(_where)/select_n | solution.py:68
  59.7 3.9 %rev.21 = s32[256,512]{1,0:T(8,128)S(1)} reverse(s32[256,512]{1,0:T(8,128)} %get-tuple-element.18), dimensions={0,1} | reverse | bytes 1048576 | tf_op jit(solution)/shard_map/rev | solution.py:69
  63.6 1.1 pad_add_fusion.1
  64.7 2.6 %copy.18 = s32[512,512]{0,1:T(8,128)} copy(s32[512,512]{1,0:T(8,128)} %pad_add_fusion.1) | data formatting | bytes 2097152 | tf_op jit(solution)/shard_map/concatenate | solution.py:70
  67.3 2.4 %fusion.9 = (s32[16,512]{1,0:T(8,128)S(1)}, bf16[512,512]{1,0:T(8,128)(2,1)S(1)}) fusion(bf16[512,512]{1,0:T(8,128)(2,1)S(1)} %get-tuple-element.21, f32[]{:T(128)} %bitcast.4, f32[512,512]{1,0:T(8,128)} %fusion.48, s32[512,512]{0,1:T(8,128)} %copy.18, s32[256,512]{1,0:T(8,128)S(1)} %rev.21, s32[256,512]{1,0:T(8,128)} %copy-done.1), kind=kOutput, calls=%fused_computation.27 | convolution fusion | flops 270786560 | bytes 4227076 | tf_op jit(solution)/shard_map/dot_general | solution.py:86
  69.7 1.9 %collective-permute-start.3 = (s32[16,512]{1,0:T(8,128)S(1)}, s32[16,512]{1,0:T(8,128)S(1)}, u32[]{:S(2)}, u32[]{:S(2)}) collective-permute-start(s32[16,512]{1,0:T(8,128)S(1)} %get-tuple-element.24), channel_id=1, source_target_pairs={{0,1},{1,2},{2,3},{3,4},{4,5},{5,6},{6,7},{7,8},{8,9},{9,10},{10,1... | collective-permute-start | bytes 98312 | tf_op jit(solution)/shard_map/ppermute | solution.py:14
  71.6 3.8 %rev.23 = s32[256,512]{1,0:T(8,128)S(1)} reverse(s32[256,512]{1,0:T(8,128)} %get-tuple-element.11), dimensions={0,1} | reverse | bytes 1048576 | tf_op jit(solution)/shard_map/rev | solution.py:69
  75.4 2.1 %pad_add_fusion.2 = s32[512,512]{1,0:T(8,128)} fusion(s32[256,512]{1,0:T(8,128)S(1)} %rev.23, s32[256,512]{1,0:T(8,128)} %get-tuple-element.10), kind=kLoop, calls=%fused_computation.23 | loop fusion | flops 262144 | bytes 2097152 | tf_op jit(solution)/shard_map/concatenate | solution.py:70
  77.5 2.5 %copy.22 = s32[512,512]{0,1:T(8,128)} copy(s32[512,512]{1,0:T(8,128)} %pad_add_fusion.2) | data formatting | bytes 2097152 | tf_op jit(solution)/shard_map/concatenate | solution.py:70
  81.4 1.5 %convert_multiply_fusion = (f32[512,512]{1,0:T(8,128)}, f32[512,512]{1,0:T(8,128)S(1)}) fusion(bf16[512,512]{1,0:T(8,128)(2,1)S(1)} %get-tuple-element.25, f32[]{:T(128)} %bitcast.4, f32[512,512]{1,0:T(8,128)S(1)} %fusion.49, s32[512,512]{0,1:T(8,128)S(1)} %copy-done.3, s32[256,512]{1,0:T(8,128)S(1)} %rev.23, s32[256,512]{1,0:T(8,128)S(1)} %copy-done), kind=kOutput, calls=%fused_computation.48 | convolution fusion | flops 270532608 | bytes 5767172 | tf_op jit(solution)/shard_map/dot_general | solution.py:86
  82.9 1.5 %convert_reduce_fusion.4 = (s32[]{:T(128)}, s32[]{:T(128)}, s32[]{:T(128)}) fusion(bf16[512,512]{1,0:T(8,128)(2,1)S(1)} %get-tuple-element.21, s32[512]{0:T(512)S(1)} %shift_right_arithmetic.162, s32[16,512]{1,0:T(8,128)S(1)} %and.71, bf16[512,512]{1,0:T(8,128)(2,1)S(1)} %get-tuple-element.25, f32[512,512]{1,0:T(8,128)S(1)} %get-tuple-element.23, f32[]{:T(128)} %bitcast.4), kind=kLoop, calls=%fused_computation.46 | loop fusion | flops 4718589 | bytes 2131984 | tf_op jit(solution)/shard_map/reduce_sum | solution.py:106
  85.3 1.5 %convert_multiply_fusion.1 = (f32[512,512]{1,0:T(8,128)}, f32[512,512]{1,0:T(8,128)S(1)}) fusion(bf16[512,512]{1,0:T(8,128)(2,1)S(1)} %fusion.6, f32[]{:T(128)} %bitcast.4, f32[512,512]{1,0:T(8,128)S(1)} %convolution_add_fusion.2, bf16[512,512]{1,0:T(8,128)(2,1)S(1)} %get-tuple-element.25), kind=kOutput, calls=%fused_computation.49 | convolution fusion | flops 269746176 | bytes 4194308 | tf_op jit(solution)/shard_map/dot_general | solution.py:79
  86.8 1.4 %convert_reduce_fusion.5 = (s32[]{:T(128)}, s32[]{:T(128)}, s32[]{:T(128)}) fusion(bf16[512,512]{1,0:T(8,128)(2,1)S(1)} %get-tuple-element.17, bf16[512,512]{1,0:T(8,128)(2,1)S(1)} %fusion.7, bf16[512,512]{1,0:T(8,128)(2,1)S(1)} %fusion.6, f32[512,512]{1,0:T(8,128)S(1)} %get-tuple-element.27, f32[]{:T(128)} %bitcast.4), kind=kLoop, calls=%fused_computation.47 | loop fusion | flops 2883581 | bytes 2621456 | tf_op jit(solution)/shard_map/reduce_sum | solution.py:105
  97.8 7.0 %all-reduce = s32[24]{0:T(128)S(1)} all-reduce(s32[24]{0:T(128)S(1)} %add_dynamic-update-slice_fusion), channel_id=2, replica_groups=mesh['rows_0'=8,'rows_1'=8,'rows_2'=4,'rows_3'=2] {'rows_0'}, use_global_device_ids=true, to_apply=%add | all-reduce | flops 24 | bytes 192
  105.2 7.0 %all-reduce.1 = s32[24]{0:T(128)S(1)} all-reduce(s32[24]{0:T(128)S(1)} %dynamic-update-slice.1), channel_id=3, replica_groups=mesh['rows_0'=8,'rows_1'=8,'rows_2'=4,'rows_3'=2] {'rows_1'}, use_global_device_ids=true, to_apply=%add.1 | all-reduce | flops 24 | bytes 192
  113.1 11.6 %all-reduce.2 = s32[12]{0:T(128)S(1)} all-reduce(s32[12]{0:T(128)S(1)} %dynamic-update-slice.2), channel_id=4, replica_groups=mesh['rows_0'=8,'rows_1'=8,'rows_2'=4,'rows_3'=2] {'rows_2'}, use_global_device_ids=true, to_apply=%add.2 | all-reduce | flops 12 | bytes 96
  125.0 8.9 %all-reduce.3 = s32[6]{0:T(128)S(1)} all-reduce(s32[6]{0:T(128)S(1)} %dynamic-update-slice.3), channel_id=5, replica_groups=mesh['rows_0'=8,'rows_1'=8,'rows_2'=4,'rows_3'=2] {'rows_3'}, use_global_device_ids=true, to_apply=%add.3 | all-reduce | flops 6 | bytes 48
  134.6 2.8 %pad_maximum_fusion = f32[512,1024]{1,0:T(8,128)} fusion(f32[512,512]{1,0:T(8,128)} %get-tuple-element.22, f32[512,512]{1,0:T(8,128)S(1)} %copy-done.2), kind=kLoop, calls=%fused_computation | loop fusion | flops 524288 | bytes 4194304 | tf_op jit(solution)/shard_map/concatenate | solution.py:126
  (64 shorter events, 13.2 us)
Async XLA Ops:
  0.6 1.4 %copy-start.4 = (s32[16,512]{1,0:T(8,128)S(1)}, s32[16,512]{1,0:T(8,128)}, u32[]{:S(2)}) copy-start(s32[16,512]{1,0:T(8,128)} %param.6) | copy-start | bytes 98308
  0.6 1.4 %copy-start.5 = (s32[16,512]{1,0:T(8,128)S(1)}, s32[16,512]{1,0:T(8,128)}, u32[]{:S(2)}) copy-start(s32[16,512]{1,0:T(8,128)} %param.8) | copy-start | bytes 98308
  3.5 20.4 %collective-permute-start.1 = (s32[8,512]{1,0:T(8,128)S(1)}, s32[8,512]{1,0:T(8,128)S(1)}, u32[]{:S(2)}, u32[]{:S(2)}) collective-permute-start(s32[8,512]{1,0:T(8,128)S(1)} %fusion.25), channel_id=1, source_target_pairs={{0,511},{1,0},{2,1},{3,2},{4,3},{5,4},{6,5},{7,6},{8,7},{9,8},{10,... | collective-permute-start | bytes 49160 | tf_op jit(solution)/shard_map/ppermute | solution.py:14
  12.6 20.0 %collective-permute-start = (s32[16,512]{1,0:T(8,128)S(1)}, s32[16,512]{1,0:T(8,128)S(1)}, u32[]{:S(2)}, u32[]{:S(2)}) collective-permute-start(s32[16,512]{1,0:T(8,128)S(1)} %get-tuple-element.9), channel_id=1, source_target_pairs={{0,1},{1,2},{2,3},{3,4},{4,5},{5,6},{6,7},{7,8},{8,9},{9,10},{10,1... | collective-permute-start | bytes 98312 | tf_op jit(solution)/shard_map/ppermute | solution.py:14
  30.7 14.6 %collective-permute-start.4 = (s32[16,512]{1,0:T(8,128)S(1)}, s32[16,512]{1,0:T(8,128)S(1)}, u32[]{:S(2)}, u32[]{:S(2)}) collective-permute-start(s32[16,512]{1,0:T(8,128)S(1)} %get-tuple-element.20), channel_id=1, source_target_pairs={{0,1},{1,2},{2,3},{3,4},{4,5},{5,6},{6,7},{7,8},{8,9},{9,10},{10,1... | collective-permute-start | bytes 98312 | tf_op jit(solution)/shard_map/ppermute | solution.py:14
  35.2 23.2 %collective-permute-start.2 = (s32[8,512]{1,0:T(8,128)S(1)}, s32[8,512]{1,0:T(8,128)S(1)}, u32[]{:S(2)}, u32[]{:S(2)}) collective-permute-start(s32[8,512]{1,0:T(8,128)S(1)} %fusion.24), channel_id=1, source_target_pairs={{0,511},{1,0},{2,1},{3,2},{4,3},{5,4},{6,5},{7,6},{8,7},{9,8},{10,... | collective-permute-start | bytes 49160 | tf_op jit(solution)/shard_map/ppermute | solution.py:14
  47.8 10.5 %collective-permute-start.5 = (s32[8,512]{1,0:T(8,128)S(1)}, s32[8,512]{1,0:T(8,128)S(1)}, u32[]{:S(2)}, u32[]{:S(2)}) collective-permute-start(s32[8,512]{1,0:T(8,128)S(1)} %fusion.23), channel_id=1, source_target_pairs={{0,511},{1,0},{2,1},{3,2},{4,3},{5,4},{6,5},{7,6},{8,7},{9,8},{10,... | collective-permute-start | bytes 49160 | tf_op jit(solution)/shard_map/ppermute | solution.py:14
  59.7 5.0 %copy-start.1 = (s32[256,512]{1,0:T(8,128)}, s32[256,512]{1,0:T(8,128)S(1)}, u32[]{:S(2)}) copy-start(s32[256,512]{1,0:T(8,128)S(1)} %get-tuple-element.19) | copy-start | bytes 1572868
  69.7 14.7 %collective-permute-start.3 = (s32[16,512]{1,0:T(8,128)S(1)}, s32[16,512]{1,0:T(8,128)S(1)}, u32[]{:S(2)}, u32[]{:S(2)}) collective-permute-start(s32[16,512]{1,0:T(8,128)S(1)} %get-tuple-element.24), channel_id=1, source_target_pairs={{0,1},{1,2},{2,3},{3,4},{4,5},{5,6},{6,7},{7,8},{8,9},{9,10},{10,1... | collective-permute-start | bytes 98312 | tf_op jit(solution)/shard_map/ppermute | solution.py:14
  80.0 1.0 copy-start
  80.0 1.4 %copy-start.3 = (s32[512,512]{0,1:T(8,128)S(1)}, s32[512,512]{0,1:T(8,128)}, u32[]{:S(2)}) copy-start(s32[512,512]{0,1:T(8,128)} %copy.22) | copy-start | bytes 3145732
  86.8 47.8 %copy-start.2 = (f32[512,512]{1,0:T(8,128)S(1)}, f32[512,512]{1,0:T(8,128)}, u32[]{:S(2)}) copy-start(f32[512,512]{1,0:T(8,128)} %get-tuple-element.26) | copy-start | bytes 3145732
